TPU v7x, 32 devices: a whole 2x2x4 slice. The times are simulated.
32 devices in a mesh: heads: 2 (over x), seq: 16 (over z, y, core).
Axes of the slice: x: 2, y: 2, z: 4, core: 2. Of those that a mesh axis runs over, the one named last changes fastest.
Arguments:
- q_nope: bfloat16 [1152, 64, 128], P('seq', 'heads'), may hold values from -6 to 6
- q_rope: bfloat16 [1152, 64, 64], P('seq', 'heads'), may hold values from -125 to 125
- latent: bfloat16 [1152, 512], P('seq'), may hold values from -6 to 6
- key_rope: bfloat16 [1152, 64], P('seq'), may hold values from -5 to 5
- absorb_key: bfloat16 [64, 128, 512], P('heads'), may hold values from -0.5 to 0.5
- absorb_value: bfloat16 [64, 512, 128], P('heads'), may hold values from -0.25 to 0.25
- w_out: bfloat16 [8192, 3584], P('heads', 'seq'), may hold values from -0.125 to 0.125
- residual: bfloat16 [1152, 3584], P(('seq', 'heads')), may hold values from -2 to 2
- norm_gain: float32 [3584], replicated, may hold values from 0.25 to 1.75
- span_table: int32 [32], replicated, may hold values from 0 to 31, each once
Outputs:
- new_residual: bfloat16 [1152, 3584], P(('seq', 'heads'))
- normed: bfloat16 [1152, 3584], P(('seq', 'heads'))
Inputs may be any that keep to these rules, and one draw needn't show every extreme that they name: `span_table`: A permutation of the span numbers.
All inputs are finite; a program needn't handle non-finite values.
Results may differ from a plain program's by a relative error of at most 0.014.
Values may be sent and summed in bfloat16 or wider, within the bound.
No kernel may reach another device: no remote copies, remote signals or barrier semaphores. Data moves between devices by JAX's collectives and lax.ppermute only.
A program may use at most 128 MiB of HBM per device.

v0:
```python
import jax
import jax.numpy as jnp
from jax import lax
from jax.sharding import PartitionSpec as P

score_scale = 192.0 ** (-0.5)


def place_rows(start, count, span_len, span_table):
    index = start + jnp.arange(count, dtype=jnp.int32)
    which = index // span_len
    picked = jnp.where(
        which[:, None] == jnp.arange(span_table.shape[0], dtype=jnp.int32)[None, :],
        span_table[None, :],
        0,
    )
    return jnp.sum(picked, axis=1) * span_len + index % span_len


def per_device(
    q_nope,
    q_rope,
    latent,
    key_rope,
    absorb_key,
    absorb_value,
    w_out,
    residual,
    norm_gain,
    span_table,
):
    tok_rows = q_nope.shape[0]
    span_len = tok_rows // 2
    seq_count = lax.axis_size("seq")
    my_start = lax.axis_index("seq") * tok_rows
    query_pos = place_rows(my_start, tok_rows, span_len, span_table)
    q_lat = jnp.einsum(
        "thd,hdl->htl", q_nope, absorb_key, preferred_element_type=jnp.float32
    ).astype(jnp.bfloat16)
    rotary = jnp.transpose(q_rope, (1, 0, 2))
    local_heads = q_lat.shape[0]

    def attend(carry, pieces, start):
        top, total, summed = carry
        lat_piece, rope_piece = pieces
        key_pos = place_rows(start, lat_piece.shape[0], span_len, span_table)
        score = jnp.einsum("htl,nl->htn", q_lat, lat_piece, preferred_element_type=jnp.float32)
        score = (
            score
            + jnp.einsum("htr,nr->htn", rotary, rope_piece, preferred_element_type=jnp.float32)
        ) * score_scale
        seen = (key_pos[None, :] <= query_pos[:, None])[None, :, :]
        score = jnp.where(seen, score, jnp.float32(-1e30))
        fresh = jnp.maximum(top, jnp.max(score, axis=2))
        weight = jnp.where(seen, jnp.exp(score - fresh[:, :, None]), jnp.float32(0.0))
        factor = jnp.exp(top - fresh)
        total = total * factor + jnp.sum(weight, axis=2)
        summed = summed * factor[:, :, None] + jnp.einsum(
            "htn,nl->htl",
            weight.astype(jnp.bfloat16),
            lat_piece,
            preferred_element_type=jnp.float32,
        )
        return (fresh, total, summed)

    start_carry = (
        jnp.full((local_heads, tok_rows), -1e30, jnp.float32),
        jnp.zeros((local_heads, tok_rows), jnp.float32),
        jnp.zeros((local_heads, tok_rows, latent.shape[1]), jnp.float32),
    )
    all_lat, all_rope = (
        lax.all_gather(latent, "seq", axis=0, tiled=True),
        lax.all_gather(key_rope, "seq", axis=0, tiled=True),
    )
    block = tok_rows * min(8, seq_count)
    steps_count = all_lat.shape[0] // block

    def visit(step, carry):
        begin = (step * block).astype(jnp.int32)
        lat_piece = lax.dynamic_slice_in_dim(all_lat, begin, block, 0)
        rope_piece = lax.dynamic_slice_in_dim(all_rope, begin, block, 0)
        return attend(carry, (lat_piece, rope_piece), begin)

    top, total, summed = lax.fori_loop(0, steps_count, visit, start_carry)
    context = (summed / total[:, :, None]).astype(jnp.bfloat16)
    per_head = jnp.einsum(
        "htl,hle->the", context, absorb_value, preferred_element_type=jnp.float32
    ).astype(jnp.bfloat16)
    heads_out = per_head.reshape(tok_rows, local_heads * per_head.shape[2])
    every_row = lax.all_gather(heads_out, "seq", axis=0, tiled=True)
    columns = jnp.dot(every_row, w_out, preferred_element_type=jnp.float32).astype(jnp.bfloat16)
    partial_value = lax.all_to_all(columns, "seq", split_axis=0, concat_axis=1, tiled=True).astype(
        jnp.float32
    )
    projected = lax.psum_scatter(
        partial_value.astype(jnp.bfloat16), "heads", scatter_dimension=0, tiled=True
    ).astype(jnp.float32)
    hidden = residual.astype(jnp.float32) + projected
    new_residual = hidden.astype(jnp.bfloat16)
    scale = lax.rsqrt(jnp.mean(hidden * hidden, axis=1, keepdims=True) + 1e-06)
    normed = (hidden * scale * norm_gain[None, :]).astype(jnp.bfloat16)
    return (new_residual, normed)


def solution(mesh):
    in_specs = (
        P("seq", "heads", None),
        P("seq", "heads", None),
        P("seq", None),
        P("seq", None),
        P("heads", None, None),
        P("heads", None, None),
        P("heads", "seq"),
        P(("seq", "heads"), None),
        P(),
        P(),
    )
    out_specs = (P(("seq", "heads"), None), P(("seq", "heads"), None))
    return jax.shard_map(
        per_device, mesh=mesh, in_specs=in_specs, out_specs=out_specs, check_vma=False
    )
```

profile of v0, /device:TPU:0, one launch (start us, length us, event | category | flops | bytes accessed | tf_op | source)
XLA Modules:
  0.0 225.6 jit_solution(14816708200302043049)
XLA Ops:
  7.2 0.7 all-gather.4.cloned.1.call-update
  8.0 24.1 %all-gather = bf16[16,72,64]{1,2,0:T(8,128)(2,1)S(1)} all-gather(bf16[1,72,64]{1,2,0:T(8,128)(2,1)} %bitcast.47), channel_id=1, replica_groups=mesh['heads'=2,'seq'=16] {'seq'}, dimensions={0}, use_global_device_ids=true | all-gather | bytes 156672 | tf_op jit(solution)/shard_map/all_gather | solution.py:73
  32.6 0.7 select_reduce_fusion.1
  33.4 4.7 %convolution_convert_fusion.1 = bf16[32,72,512]{2,1,0:T(8,128)(2,1)} fusion(bf16[32,128,512]{2,1,0:T(8,128)(2,1)} %param.16, bf16[72,32,128]{2,1,0:T(8,128)(2,1)} %param.12), kind=kOutput, calls=%fused_computation.41 | convolution fusion | flops 303169536 | bytes 7143424 | tf_op jit(solution)/shard_map/thd,hdl->htl/dot_general | solution.py:37
  38.0 13.4 %all-gather.4.cloned.1.call-done = bf16[1152,512]{1,0:T(8,128)(2,1)} async-done(((bf16[72,512]{1,0:T(8,128)(2,1)}), bf16[1152,512]{1,0:T(8,128)(2,1)}) %all-gather.4.cloned.1.call-update) | async-done | bytes 1179664 | tf_op jit(solution)/shard_map/all_gather | solution.py:72
  51.4 36.1 %while.20 = (s32[]{:T(128)}, f32[32,72]{1,0:T(8,128)S(1)}, f32[32,72]{1,0:T(8,128)S(1)}, f32[32,72,512]{2,1,0:T(8,128)}, s32[32]{0:T(128)S(1)}, /*index=5*/s32[7...) while((s32[]{:T(128)}, f32[32,72]{1,0:T(8,128)S(1)}, ...), condition=%wide.region_5.6_spmd.clone, body=%wide.region_1.5_spmd.clone.sunk | while | flops 2904706304 | bytes 68787400 | solution.py:84
  51.4 3.9 %fusion.59 = f32[576,32,72]{0,2,1:T(8,128)S(1)} fusion(bf16[32,72,512]{2,1,0:T(8,128)(2,1)} %get-tuple-element.413, bf16[1152,512]{1,0:T(8,128)(2,1)} %get-tuple-element.412, s32[]{:T(128)S(6)} %select_n.141), kind=kOutput, calls=%fused_computation.11.clone.1 | convolution fusion | flops 1358954496 | bytes 8257540 | tf_op jit(solution)/shard_map/while/body/eval_jaxpr/htl,nl->htn/dot_general | solution.py:47
  55.6 4.2 %fusion.61 = (f32[32,72]{1,0:T(8,128)S(1)}, f32[32,72,576]{2,1,0:T(8,128)}) fusion(f32[576,32,72]{0,2,1:T(8,128)S(1)} %fusion.59, bf16[32,72,64]{1,2,0:T(8,128)(2,1)S(1)} %copy-done.3, bf16[1152,64]{0,1:T(8,128)(2,1)S(1)} %get-tuple-element.414, s32[]{:T(128)S(6)} %select_n.141, pred[72,576]{1,0:T(8,128)(4,1)S(1)} %broadcast_compare_fusion.2), kind=kOutput, calls=%fused_computation.58.clone.1 | convolution fusion | flops 175175424 | bytes 11868164 | tf_op jit(solution)/shard_map/while/body/eval_jaxpr/htr,nr->htn/dot_general | solution.py:50
  59.9 4.1 %fusion.62 = f32[32,72]{1,0:T(8,128)S(1)} fusion(f32[32,72,576]{2,1,0:T(8,128)} %get-tuple-element.375, f32[32,72]{1,0:T(8,128)S(1)} %select_maximum_fusion.2, pred[72,576]{1,0:T(8,128)(4,1)S(1)} %broadcast_compare_fusion.2), kind=kLoop, calls=%fused_computation.3.clone.1 | loop fusion | flops 3979008 | bytes 5368320 | tf_op jit(solution)/shard_map/while/body/eval_jaxpr/reduce_sum | solution.py:57
  64.3 4.4 %fusion.64 = f32[32,72,512]{2,1,0:T(8,128)} fusion(f32[32,72,512]{2,1,0:T(8,128)} %get-tuple-element.395, f32[32,72]{1,0:T(8,128)S(1)} %get-tuple-element.377, pred[]{:T(512)S(6)} %compare.3, f32[32,72,576]{2,1,0:T(8,128)S(1)} %copy-done.1, f32[32,72]{1,0:T(8,128)S(1)} %select_maximum_fusion.2, pred[72,576]{1,0:T(8,128)(4,1)S(1)} %broadcast_compare_fusion.2, ...), kind=kOutput, calls=%fused_computation.5.clone.1 | convolution fusion | flops 1366474752 | bytes 16004101 | tf_op jit(solution)/shard_map/while/body/eval_jaxpr/htn,nl->htl/dot_general | solution.py:58
  68.6 3.9 %fusion.59 = f32[576,32,72]{0,2,1:T(8,128)S(1)} fusion(bf16[32,72,512]{2,1,0:T(8,128)(2,1)} %get-tuple-element.413, bf16[1152,512]{1,0:T(8,128)(2,1)} %get-tuple-element.412, s32[]{:T(128)S(6)} %select_n.141), kind=kOutput, calls=%fused_computation.11.clone.1 | convolution fusion | flops 1358954496 | bytes 8257540 | tf_op jit(solution)/shard_map/while/body/eval_jaxpr/htl,nl->htn/dot_general | solution.py:47
  72.8 4.2 %fusion.61 = (f32[32,72]{1,0:T(8,128)S(1)}, f32[32,72,576]{2,1,0:T(8,128)}) fusion(f32[576,32,72]{0,2,1:T(8,128)S(1)} %fusion.59, bf16[32,72,64]{1,2,0:T(8,128)(2,1)S(1)} %copy-done.3, bf16[1152,64]{0,1:T(8,128)(2,1)S(1)} %get-tuple-element.414, s32[]{:T(128)S(6)} %select_n.141, pred[72,576]{1,0:T(8,128)(4,1)S(1)} %broadcast_compare_fusion.2), kind=kOutput, calls=%fused_computation.58.clone.1 | convolution fusion | flops 175175424 | bytes 11868164 | tf_op jit(solution)/shard_map/while/body/eval_jaxpr/htr,nr->htn/dot_general | solution.py:50
  77.1 4.1 %fusion.62 = f32[32,72]{1,0:T(8,128)S(1)} fusion(f32[32,72,576]{2,1,0:T(8,128)} %get-tuple-element.375, f32[32,72]{1,0:T(8,128)S(1)} %select_maximum_fusion.2, pred[72,576]{1,0:T(8,128)(4,1)S(1)} %broadcast_compare_fusion.2), kind=kLoop, calls=%fused_computation.3.clone.1 | loop fusion | flops 3979008 | bytes 5368320 | tf_op jit(solution)/shard_map/while/body/eval_jaxpr/reduce_sum | solution.py:57
  81.5 6.0 %fusion.64 = f32[32,72,512]{2,1,0:T(8,128)} fusion(f32[32,72,512]{2,1,0:T(8,128)} %get-tuple-element.395, f32[32,72]{1,0:T(8,128)S(1)} %get-tuple-element.377, pred[]{:T(512)S(6)} %compare.3, f32[32,72,576]{2,1,0:T(8,128)S(1)} %copy-done.1, f32[32,72]{1,0:T(8,128)S(1)} %select_maximum_fusion.2, pred[72,576]{1,0:T(8,128)(4,1)S(1)} %broadcast_compare_fusion.2, ...), kind=kOutput, calls=%fused_computation.5.clone.1 | convolution fusion | flops 1366474752 | bytes 16004101 | tf_op jit(solution)/shard_map/while/body/eval_jaxpr/htn,nl->htl/dot_general | solution.py:58
  87.5 4.6 %fusion.31 = bf16[32,9,8,128]{3,2,1,0:T(8,128)(2,1)S(1)} fusion(bf16[32,512,128]{2,1,0:T(8,128)(2,1)} %param.17, f32[32,72,512]{2,1,0:T(8,128)} %get-tuple-element.248, f32[32,72]{1,0:T(8,128)S(1)} %get-tuple-element.249), kind=kOutput, calls=%fused_computation.43 | convolution fusion | flops 304644096 | bytes 9511936 | tf_op jit(solution)/shard_map/htl,hle->the/dot_general | solution.py:86
  92.1 0.9 copy.42
  93.1 79.9 %all-gather.6.cloned.1.call-done = bf16[1152,4096]{1,0:T(8,128)(2,1)} async-done(((bf16[72,4096]{1,0:T(8,128)(2,1)}), bf16[1152,4096]{1,0:T(8,128)(2,1)}) %all-gather.6.cloned.1.call-update) | async-done | bytes 9437200 | tf_op jit(solution)/shard_map/all_gather | solution.py:90
  173.0 6.7 %convolution_convert_fusion = bf16[1152,224]{0,1:T(8,128)(2,1)S(1)} fusion(bf16[1152,4096]{1,0:T(8,128)(2,1)} %all-gather.6.cloned.1.call-done, bf16[4096,224]{0,1:T(8,128)(2,1)S(1)} %copy-done), kind=kOutput, calls=%fused_computation.39 | convolution fusion | flops 2114187264 | bytes 11788288 | tf_op jit(solution)/shard_map/dot_general | solution.py:91
  180.0 20.2 %all_to_all.19 = bf16[16,72,224]{2,1,0:T(8,128)(2,1)S(1)} all-to-all(bf16[16,72,224]{2,1,0:T(8,128)(2,1)S(1)} %bitcast.45), channel_id=1, replica_groups=mesh['heads'=2,'seq'=16] {'seq'}, dimensions={0} | all-to-all | bytes 1032192 | tf_op jit(solution)/shard_map/all_to_all | solution.py:92
  200.3 1.0 all_to_all.17
  201.3 11.8 %fusion = bf16[40,3584]{1,0:T(8,128)(2,1)S(1)} fusion(bf16[72,3584]{1,0:T(8,128)(2,1)S(1)} %all_to_all.17), kind=kCustom, calls=%all-reduce-scatter | all-reduce-scatter fusion | flops 286721 | bytes 803328
  213.1 2.5 %collective-permute-start = (bf16[4,3584]{1,0:T(4,128)(2,1)S(1)}, bf16[4,3584]{1,0:T(4,128)(2,1)S(1)}, u32[]{:S(2)}, u32[]{:S(2)}) collective-permute-start(bf16[4,3584]{1,0:T(4,128)(2,1)S(1)} %slice), channel_id=1, source_target_pairs={{0,16},{1,17},{2,18},{3,19},{4,20},{5,21},{6,22},{7,23},{8,24},{9,... | collective-permute-start | bytes 86024
  215.6 0.6 dynamic-slice.4
  217.8 1.0 multiply_convert_fusion
  (53 shorter events, 3.0 us)
Async XLA Ops:
  7.2 165.8 %copy-start = (bf16[4096,224]{0,1:T(8,128)(2,1)S(1)}, bf16[4096,224]{0,1:T(8,128)(2,1)}, u32[]{:S(2)}) copy-start(bf16[4096,224]{0,1:T(8,128)(2,1)} %param.18) | copy-start | bytes 5505028
  7.2 44.2 %copy-start.6 = (s32[32]{0:T(128)S(1)}, s32[32]{0:T(128)}, u32[]{:S(2)}) copy-start(s32[32]{0:T(128)} %param.21) | copy-start | bytes 388
  7.2 44.2 %all-gather.4.cloned.1.call-start = ((), (), s32[]{:S(2)}) async-start(), calls=%async_computation.1 | async-start | bytes 1253376 | tf_op jit(solution)/shard_map/all_gather | solution.py:72
  7.9 165.1 %all-gather.6.cloned.1.call-start = ((), (), s32[]{:S(2)}) async-start(), calls=%async_computation.2 | async-start | bytes 10027008 | tf_op jit(solution)/shard_map/all_gather | solution.py:90
  51.4 4.2 %copy-start.3 = (bf16[32,72,64]{1,2,0:T(8,128)(2,1)S(1)}, bf16[32,72,64]{1,2,0:T(8,128)(2,1)}, u32[]{:S(2)}) copy-start(bf16[32,72,64]{1,2,0:T(8,128)(2,1)} %get-tuple-element.415) | copy-start | bytes 884740 | tf_op jit(solution)/shard_map/while
  55.6 8.4 %copy-start.2 = (bf16[1152,512]{1,0:T(8,128)(2,1)S(1)}, bf16[1152,512]{1,0:T(8,128)(2,1)}, u32[]{:S(2)}) copy-start(bf16[1152,512]{1,0:T(8,128)(2,1)} %get-tuple-element.412) | copy-start | bytes 3538948 | tf_op jit(solution)/shard_map/while
  59.8 4.4 %copy-start.1 = (f32[32,72,576]{2,1,0:T(8,128)S(1)}, f32[32,72,576]{2,1,0:T(8,128)}, u32[]{:S(2)}) copy-start(f32[32,72,576]{2,1,0:T(8,128)} %get-tuple-element.375) | copy-start | bytes 15925252 | tf_op jit(solution)/shard_map/while
  68.6 4.2 %copy-start.3 = (bf16[32,72,64]{1,2,0:T(8,128)(2,1)S(1)}, bf16[32,72,64]{1,2,0:T(8,128)(2,1)}, u32[]{:S(2)}) copy-start(bf16[32,72,64]{1,2,0:T(8,128)(2,1)} %get-tuple-element.415) | copy-start | bytes 884740 | tf_op jit(solution)/shard_map/while
  72.8 8.4 %copy-start.2 = (bf16[1152,512]{1,0:T(8,128)(2,1)S(1)}, bf16[1152,512]{1,0:T(8,128)(2,1)}, u32[]{:S(2)}) copy-start(bf16[1152,512]{1,0:T(8,128)(2,1)} %get-tuple-element.412) | copy-start | bytes 3538948 | tf_op jit(solution)/shard_map/while
  77.1 4.4 %copy-start.1 = (f32[32,72,576]{2,1,0:T(8,128)S(1)}, f32[32,72,576]{2,1,0:T(8,128)}, u32[]{:S(2)}) copy-start(f32[32,72,576]{2,1,0:T(8,128)} %get-tuple-element.375) | copy-start | bytes 15925252 | tf_op jit(solution)/shard_map/while
  179.8 35.8 %copy-start.7 = (u32[32]{0:T(128)S(1)}, u32[32]{0:T(128)}, u32[]{:S(2)}) copy-start(u32[32]{0:T(128)} %constant.152) | copy-start | bytes 388
  179.8 37.8 %copy-start.4 = (bf16[36,3584]{1,0:T(8,128)(2,1)S(1)}, bf16[36,3584]{1,0:T(8,128)(2,1)}, u32[]{:S(2)}) copy-start(bf16[36,3584]{1,0:T(8,128)(2,1)} %param.19) | copy-start | bytes 774148
  179.8 38.0 %copy-start.5 = (f32[3584]{0:T(1024)S(1)}, f32[3584]{0:T(1024)}, u32[]{:S(2)}) copy-start(f32[3584]{0:T(1024)} %param.20) | copy-start | bytes 43012
  213.1 4.0 %collective-permute-start = (bf16[4,3584]{1,0:T(4,128)(2,1)S(1)}, bf16[4,3584]{1,0:T(4,128)(2,1)S(1)}, u32[]{:S(2)}, u32[]{:S(2)}) collective-permute-start(bf16[4,3584]{1,0:T(4,128)(2,1)S(1)} %slice), channel_id=1, source_target_pairs={{0,16},{1,17},{2,18},{3,19},{4,20},{5,21},{6,22},{7,23},{8,24},{9,... | collective-permute-start | bytes 86024
Sparse Core Ops, SparseCore 0:
  10.3 41.0 all-gather.3
  93.2 79.7 all-gather.5
where the time goes:
time: 226 us
  waiting for transfers between devices  94.3 us (42%)
  blocking collectives  56.1 us (25%)
  matrix products  42.8 us (19%)
  between operations  14.9 us (7%)
  other arithmetic  10.7 us (5%)
  local copies, waits for them, and re-layouts  4.29 us (2%)
  starting transfers between devices  2.54 us (1%)
    all_gather x1, waiting for transfers between devices, per_device(): every_row = lax.all_gather(heads_out, 'seq', axis=0, tiled=True)  79.9 us
    all_gather x1, blocking collectives, per_device(): lax.all_gather(key_rope, 'seq', axis=0, tiled=True)  24.1 us
    all_to_all x1, blocking collectives, per_device(): lax.all_to_all(columns, 'seq', split_axis=0, concat_axis=1, tiled=True)  20.2 us
    all_gather x1, waiting for transfers between devices, per_device(): lax.all_gather(latent, 'seq', axis=0, tiled=True)  13.4 us
    unnamed x1, blocking collectives  11.8 us
    dot_general x2, matrix products, attend(): jnp.einsum('htn,nl->htl', weight.astype(jnp.bfloat16), lat_piece, preferr...  10.4 us
    dot_general x2, matrix products, attend(): jnp.einsum('htr,nr->htn', rotary, rope_piece, preferred_element_type=jnp....  8.46 us
    reduce_sum x2, other arithmetic, attend(): total = total * factor + jnp.sum(weight, axis=2)  8.21 us
  transfers between devices with their start and end apart: 3, of which 3 were waited for; matrix products, arithmetic and copies ran while one was open for 3% of the time, Pallas kernels for 0%

commit v1 on v0

--- a/solution.py
+++ b/solution.py
@@ -70,7 +70,9 @@
     )
     all_lat, all_rope = (
         lax.all_gather(latent, "seq", axis=0, tiled=True),
-        lax.all_gather(key_rope, "seq", axis=0, tiled=True),
+        jnp.concatenate(
+            lax.all_to_all(jnp.stack([key_rope] * lax.axis_size("seq")), "seq", 0, 0), axis=0
+        ),
     )
     block = tok_rows * min(8, seq_count)
     steps_count = all_lat.shape[0] // block

time: 226 us -> 227 us (level)
  blocking collectives: 56.1 us -> 31.9 us
  waiting for transfers between devices: 94.3 us -> 111 us
  starting transfers between devices: 2.54 us -> 9.96 us
    all_gather x1 -> x0, blocking collectives: 24.1 us -> none  [per_device(): lax.all_gather(key_rope, 'seq', axis=0, tiled=True)]
    all_gather x1, waiting for transfers between devices: 13.4 us -> 24.1 us  [per_device(): lax.all_gather(latent, 'seq', axis=0, tiled=True)]
    all_to_all x0 -> x1, starting transfers between devices: none -> 7.41 us  [per_device(): lax.all_to_all(jnp.stack([key_rope] * lax.axis_size('seq')), 'seq', 0, 0)]
    all_to_all x0 -> x1, waiting for transfers between devices: none -> 5.84 us  [per_device(): lax.all_to_all(jnp.stack([key_rope] * lax.axis_size('seq')), 'seq', 0, 0)]
  transfers between devices with their start and end apart: 3 -> 4, of which waited for: 3 -> 4; matrix products, arithmetic and copies ran while one was open for 3% -> 3% of each run, Pallas kernels for 0% -> 0%
where the time goes in v1:
time: 227 us; the launch traced here: 226 us
  waiting for transfers between devices  111 us (49%)
  matrix products  42.8 us (19%)
  blocking collectives  31.9 us (14%)
  between operations  14.9 us (7%)
  starting transfers between devices  9.96 us (4%)
  other arithmetic  9.94 us (4%)
  local copies, waits for them, and re-layouts  5.84 us (3%)
    all_gather x1, waiting for transfers between devices, per_device(): every_row = lax.all_gather(heads_out, 'seq', axis=0, tiled=True)  79.9 us
    all_gather x1, waiting for transfers between devices, per_device(): lax.all_gather(latent, 'seq', axis=0, tiled=True)  24.1 us
    all_to_all x1, blocking collectives, per_device(): lax.all_to_all(columns, 'seq', split_axis=0, concat_axis=1, tiled=True)  20.2 us
    unnamed x1, blocking collectives  11.8 us
    dot_general x2, matrix products, attend(): jnp.einsum('htn,nl->htl', weight.astype(jnp.bfloat16), lat_piece, preferr...  10.4 us
    dot_general x2, matrix products, attend(): jnp.einsum('htr,nr->htn', rotary, rope_piece, preferred_element_type=jnp....  8.48 us
    reduce_sum x2, other arithmetic, attend(): total = total * factor + jnp.sum(weight, axis=2)  8.14 us
    dot_general x2, matrix products, attend(): jnp.einsum('htl,nl->htn', q_lat, lat_piece, preferred_element_type=jnp.fl...  7.9 us
  transfers between devices with their start and end apart: 4, of which 4 were waited for; matrix products, arithmetic and copies ran while one was open for 3% of the time, Pallas kernels for 0%

profile of v1, /device:TPU:0, one launch (start us, length us, event | category | flops | bytes accessed | tf_op | source)
XLA Modules:
  0.0 226.3 jit_solution(7772394258128054134)
XLA Ops:
  7.2 0.7 all-gather.3.cloned.1.call-update
  7.9 1.5 stack.2
  9.4 7.4 %all-to-all-start = ((bf16[16,72,64]{1,2,0:T(8,128)(2,1)}), bf16[16,72,64]{1,2,0:T(8,128)(2,1)S(1)}, u32[]{:S(2)}, u32[]{:S(2)}) async-start(bf16[16,72,64]{1,2,0:T(8,128)(2,1)} %stack.2), calls=%async_computation | async-start | bytes 524288 | tf_op jit(solution)/shard_map/all_to_all | solution.py:74
  16.9 4.7 %convolution_convert_fusion.1 = bf16[32,72,512]{2,1,0:T(8,128)(2,1)} fusion(bf16[32,128,512]{2,1,0:T(8,128)(2,1)} %param.16, bf16[72,32,128]{2,1,0:T(8,128)(2,1)} %param.12), kind=kOutput, calls=%fused_computation.41 | convolution fusion | flops 303169536 | bytes 7143424 | tf_op jit(solution)/shard_map/thd,hdl->htl/dot_general | solution.py:37
  21.7 5.8 %all-to-all-done = bf16[16,72,64]{1,2,0:T(8,128)(2,1)S(1)} async-done(((bf16[16,72,64]{1,2,0:T(8,128)(2,1)}), bf16[16,72,64]{1,2,0:T(8,128)(2,1)S(1)}, u32[]{:S(2)}, u32[]{:S(2)}) %all-to-all-start) | async-done | bytes 147488 | tf_op jit(solution)/shard_map/all_to_all | solution.py:74
  28.0 24.1 %all-gather.3.cloned.1.call-done = bf16[1152,512]{1,0:T(8,128)(2,1)} async-done(((bf16[72,512]{1,0:T(8,128)(2,1)}), bf16[1152,512]{1,0:T(8,128)(2,1)}) %all-gather.3.cloned.1.call-update) | async-done | bytes 1179664 | tf_op jit(solution)/shard_map/all_gather | solution.py:72
  52.1 36.1 %while.20 = (s32[]{:T(128)}, f32[32,72]{1,0:T(8,128)S(1)}, f32[32,72]{1,0:T(8,128)S(1)}, f32[32,72,512]{2,1,0:T(8,128)}, s32[32]{0:T(128)S(1)}, /*index=5*/s32[7...) while((s32[]{:T(128)}, f32[32,72]{1,0:T(8,128)S(1)}, ...), condition=%wide.region_5.6_spmd.clone, body=%wide.region_1.5_spmd.clone.sunk | while | flops 2904706304 | bytes 68787400 | solution.py:86
  52.1 3.9 %fusion.59 = f32[576,32,72]{0,2,1:T(8,128)S(1)} fusion(bf16[32,72,512]{2,1,0:T(8,128)(2,1)} %get-tuple-element.413, bf16[1152,512]{1,0:T(8,128)(2,1)} %get-tuple-element.412, s32[]{:T(128)S(6)} %select_n.141), kind=kOutput, calls=%fused_computation.11.clone.1 | convolution fusion | flops 1358954496 | bytes 8257540 | tf_op jit(solution)/shard_map/while/body/eval_jaxpr/htl,nl->htn/dot_general | solution.py:47
  56.3 4.2 %fusion.61 = (f32[32,72]{1,0:T(8,128)S(1)}, f32[32,72,576]{2,1,0:T(8,128)}) fusion(f32[576,32,72]{0,2,1:T(8,128)S(1)} %fusion.59, bf16[32,72,64]{1,2,0:T(8,128)(2,1)S(1)} %copy-done.3, bf16[1152,64]{0,1:T(8,128)(2,1)S(1)} %get-tuple-element.414, s32[]{:T(128)S(6)} %select_n.141, pred[72,576]{1,0:T(8,128)(4,1)S(1)} %broadcast_compare_fusion.2), kind=kOutput, calls=%fused_computation.58.clone.1 | convolution fusion | flops 175175424 | bytes 11868164 | tf_op jit(solution)/shard_map/while/body/eval_jaxpr/htr,nr->htn/dot_general | solution.py:50
  60.5 4.1 %fusion.62 = f32[32,72]{1,0:T(8,128)S(1)} fusion(f32[32,72,576]{2,1,0:T(8,128)} %get-tuple-element.375, f32[32,72]{1,0:T(8,128)S(1)} %select_maximum_fusion.2, pred[72,576]{1,0:T(8,128)(4,1)S(1)} %broadcast_compare_fusion.2), kind=kLoop, calls=%fused_computation.3.clone.1 | loop fusion | flops 3979008 | bytes 5368320 | tf_op jit(solution)/shard_map/while/body/eval_jaxpr/reduce_sum | solution.py:57
  64.9 4.4 %fusion.64 = f32[32,72,512]{2,1,0:T(8,128)} fusion(f32[32,72,512]{2,1,0:T(8,128)} %get-tuple-element.395, f32[32,72]{1,0:T(8,128)S(1)} %get-tuple-element.377, pred[]{:T(512)S(6)} %compare.3, f32[32,72,576]{2,1,0:T(8,128)S(1)} %copy-done.1, f32[32,72]{1,0:T(8,128)S(1)} %select_maximum_fusion.2, pred[72,576]{1,0:T(8,128)(4,1)S(1)} %broadcast_compare_fusion.2, ...), kind=kOutput, calls=%fused_computation.5.clone.1 | convolution fusion | flops 1366474752 | bytes 16004101 | tf_op jit(solution)/shard_map/while/body/eval_jaxpr/htn,nl->htl/dot_general | solution.py:58
  69.3 3.9 %fusion.59 = f32[576,32,72]{0,2,1:T(8,128)S(1)} fusion(bf16[32,72,512]{2,1,0:T(8,128)(2,1)} %get-tuple-element.413, bf16[1152,512]{1,0:T(8,128)(2,1)} %get-tuple-element.412, s32[]{:T(128)S(6)} %select_n.141), kind=kOutput, calls=%fused_computation.11.clone.1 | convolution fusion | flops 1358954496 | bytes 8257540 | tf_op jit(solution)/shard_map/while/body/eval_jaxpr/htl,nl->htn/dot_general | solution.py:47
  73.5 4.2 %fusion.61 = (f32[32,72]{1,0:T(8,128)S(1)}, f32[32,72,576]{2,1,0:T(8,128)}) fusion(f32[576,32,72]{0,2,1:T(8,128)S(1)} %fusion.59, bf16[32,72,64]{1,2,0:T(8,128)(2,1)S(1)} %copy-done.3, bf16[1152,64]{0,1:T(8,128)(2,1)S(1)} %get-tuple-element.414, s32[]{:T(128)S(6)} %select_n.141, pred[72,576]{1,0:T(8,128)(4,1)S(1)} %broadcast_compare_fusion.2), kind=kOutput, calls=%fused_computation.58.clone.1 | convolution fusion | flops 175175424 | bytes 11868164 | tf_op jit(solution)/shard_map/while/body/eval_jaxpr/htr,nr->htn/dot_general | solution.py:50
  77.8 4.1 %fusion.62 = f32[32,72]{1,0:T(8,128)S(1)} fusion(f32[32,72,576]{2,1,0:T(8,128)} %get-tuple-element.375, f32[32,72]{1,0:T(8,128)S(1)} %select_maximum_fusion.2, pred[72,576]{1,0:T(8,128)(4,1)S(1)} %broadcast_compare_fusion.2), kind=kLoop, calls=%fused_computation.3.clone.1 | loop fusion | flops 3979008 | bytes 5368320 | tf_op jit(solution)/shard_map/while/body/eval_jaxpr/reduce_sum | solution.py:57
  82.2 6.0 %fusion.64 = f32[32,72,512]{2,1,0:T(8,128)} fusion(f32[32,72,512]{2,1,0:T(8,128)} %get-tuple-element.395, f32[32,72]{1,0:T(8,128)S(1)} %get-tuple-element.377, pred[]{:T(512)S(6)} %compare.3, f32[32,72,576]{2,1,0:T(8,128)S(1)} %copy-done.1, f32[32,72]{1,0:T(8,128)S(1)} %select_maximum_fusion.2, pred[72,576]{1,0:T(8,128)(4,1)S(1)} %broadcast_compare_fusion.2, ...), kind=kOutput, calls=%fused_computation.5.clone.1 | convolution fusion | flops 1366474752 | bytes 16004101 | tf_op jit(solution)/shard_map/while/body/eval_jaxpr/htn,nl->htl/dot_general | solution.py:58
  88.2 4.6 %fusion.31 = bf16[32,9,8,128]{3,2,1,0:T(8,128)(2,1)S(1)} fusion(bf16[32,512,128]{2,1,0:T(8,128)(2,1)} %param.17, f32[32,72,512]{2,1,0:T(8,128)} %get-tuple-element.248, f32[32,72]{1,0:T(8,128)S(1)} %get-tuple-element.249), kind=kOutput, calls=%fused_computation.43 | convolution fusion | flops 304644096 | bytes 9511936 | tf_op jit(solution)/shard_map/htl,hle->the/dot_general | solution.py:88
  92.8 0.9 copy.39
  93.8 79.9 %all-gather.5.cloned.1.call-done = bf16[1152,4096]{1,0:T(8,128)(2,1)} async-done(((bf16[72,4096]{1,0:T(8,128)(2,1)}), bf16[1152,4096]{1,0:T(8,128)(2,1)}) %all-gather.5.cloned.1.call-update) | async-done | bytes 9437200 | tf_op jit(solution)/shard_map/all_gather | solution.py:92
  173.7 6.7 %convolution_convert_fusion = bf16[1152,224]{0,1:T(8,128)(2,1)S(1)} fusion(bf16[1152,4096]{1,0:T(8,128)(2,1)} %all-gather.5.cloned.1.call-done, bf16[4096,224]{0,1:T(8,128)(2,1)S(1)} %copy-done), kind=kOutput, calls=%fused_computation.39 | convolution fusion | flops 2114187264 | bytes 11788288 | tf_op jit(solution)/shard_map/dot_general | solution.py:93
  180.8 20.2 %all_to_all.24 = bf16[16,72,224]{2,1,0:T(8,128)(2,1)S(1)} all-to-all(bf16[16,72,224]{2,1,0:T(8,128)(2,1)S(1)} %bitcast.44), channel_id=1, replica_groups=mesh['heads'=2,'seq'=16] {'seq'}, dimensions={0} | all-to-all | bytes 1032192 | tf_op jit(solution)/shard_map/all_to_all | solution.py:94
  201.0 1.0 all_to_all.21
  202.0 11.8 %fusion = bf16[40,3584]{1,0:T(8,128)(2,1)S(1)} fusion(bf16[72,3584]{1,0:T(8,128)(2,1)S(1)} %all_to_all.21), kind=kCustom, calls=%all-reduce-scatter | all-reduce-scatter fusion | flops 286721 | bytes 803328
  213.8 2.5 %collective-permute-start = (bf16[4,3584]{1,0:T(4,128)(2,1)S(1)}, bf16[4,3584]{1,0:T(4,128)(2,1)S(1)}, u32[]{:S(2)}, u32[]{:S(2)}) collective-permute-start(bf16[4,3584]{1,0:T(4,128)(2,1)S(1)} %slice), channel_id=1, source_target_pairs={{0,16},{1,17},{2,18},{3,19},{4,20},{5,21},{6,22},{7,23},{8,24},{9,... | collective-permute-start | bytes 86024
  218.5 1.0 multiply_convert_fusion
  (55 shorter events, 3.7 us)
Async XLA Ops:
  7.2 166.6 %copy-start = (bf16[4096,224]{0,1:T(8,128)(2,1)S(1)}, bf16[4096,224]{0,1:T(8,128)(2,1)}, u32[]{:S(2)}) copy-start(bf16[4096,224]{0,1:T(8,128)(2,1)} %param.18) | copy-start | bytes 5505028
  7.2 14.4 %copy-start.6 = (s32[32]{0:T(128)S(1)}, s32[32]{0:T(128)}, u32[]{:S(2)}) copy-start(s32[32]{0:T(128)} %param.21) | copy-start | bytes 388
  7.2 44.9 %all-gather.3.cloned.1.call-start = ((), (), s32[]{:S(2)}) async-start(), calls=%async_computation.2 | async-start | bytes 1253376 | tf_op jit(solution)/shard_map/all_gather | solution.py:72
  9.4 18.1 %all-to-all-start = ((bf16[16,72,64]{1,2,0:T(8,128)(2,1)}), bf16[16,72,64]{1,2,0:T(8,128)(2,1)S(1)}, u32[]{:S(2)}, u32[]{:S(2)}) async-start(bf16[16,72,64]{1,2,0:T(8,128)(2,1)} %stack.2), calls=%async_computation | async-start | bytes 524288 | tf_op jit(solution)/shard_map/all_to_all | solution.py:74
  16.8 156.9 %all-gather.5.cloned.1.call-start = ((), (), s32[]{:S(2)}) async-start(), calls=%async_computation.3 | async-start | bytes 10027008 | tf_op jit(solution)/shard_map/all_gather | solution.py:92
  52.1 4.2 %copy-start.3 = (bf16[32,72,64]{1,2,0:T(8,128)(2,1)S(1)}, bf16[32,72,64]{1,2,0:T(8,128)(2,1)}, u32[]{:S(2)}) copy-start(bf16[32,72,64]{1,2,0:T(8,128)(2,1)} %get-tuple-element.415) | copy-start | bytes 884740 | tf_op jit(solution)/shard_map/while
  56.3 8.4 %copy-start.2 = (bf16[1152,512]{1,0:T(8,128)(2,1)S(1)}, bf16[1152,512]{1,0:T(8,128)(2,1)}, u32[]{:S(2)}) copy-start(bf16[1152,512]{1,0:T(8,128)(2,1)} %get-tuple-element.412) | copy-start | bytes 3538948 | tf_op jit(solution)/shard_map/while
  60.5 4.4 %copy-start.1 = (f32[32,72,576]{2,1,0:T(8,128)S(1)}, f32[32,72,576]{2,1,0:T(8,128)}, u32[]{:S(2)}) copy-start(f32[32,72,576]{2,1,0:T(8,128)} %get-tuple-element.375) | copy-start | bytes 15925252 | tf_op jit(solution)/shard_map/while
  69.3 4.2 %copy-start.3 = (bf16[32,72,64]{1,2,0:T(8,128)(2,1)S(1)}, bf16[32,72,64]{1,2,0:T(8,128)(2,1)}, u32[]{:S(2)}) copy-start(bf16[32,72,64]{1,2,0:T(8,128)(2,1)} %get-tuple-element.415) | copy-start | bytes 884740 | tf_op jit(solution)/shard_map/while
  73.5 8.4 %copy-start.2 = (bf16[1152,512]{1,0:T(8,128)(2,1)S(1)}, bf16[1152,512]{1,0:T(8,128)(2,1)}, u32[]{:S(2)}) copy-start(bf16[1152,512]{1,0:T(8,128)(2,1)} %get-tuple-element.412) | copy-start | bytes 3538948 | tf_op jit(solution)/shard_map/while
  77.8 4.4 %copy-start.1 = (f32[32,72,576]{2,1,0:T(8,128)S(1)}, f32[32,72,576]{2,1,0:T(8,128)}, u32[]{:S(2)}) copy-start(f32[32,72,576]{2,1,0:T(8,128)} %get-tuple-element.375) | copy-start | bytes 15925252 | tf_op jit(solution)/shard_map/while
  180.5 35.8 %copy-start.7 = (u32[32]{0:T(128)S(1)}, u32[32]{0:T(128)}, u32[]{:S(2)}) copy-start(u32[32]{0:T(128)} %constant.152) | copy-start | bytes 388
  180.5 37.8 %copy-start.4 = (bf16[36,3584]{1,0:T(8,128)(2,1)S(1)}, bf16[36,3584]{1,0:T(8,128)(2,1)}, u32[]{:S(2)}) copy-start(bf16[36,3584]{1,0:T(8,128)(2,1)} %param.19) | copy-start | bytes 774148
  180.5 38.0 %copy-start.5 = (f32[3584]{0:T(1024)S(1)}, f32[3584]{0:T(1024)}, u32[]{:S(2)}) copy-start(f32[3584]{0:T(1024)} %param.20) | copy-start | bytes 43012
  213.8 4.0 %collective-permute-start = (bf16[4,3584]{1,0:T(4,128)(2,1)S(1)}, bf16[4,3584]{1,0:T(4,128)(2,1)S(1)}, u32[]{:S(2)}, u32[]{:S(2)}) collective-permute-start(bf16[4,3584]{1,0:T(4,128)(2,1)S(1)} %slice), channel_id=1, source_target_pairs={{0,16},{1,17},{2,18},{3,19},{4,20},{5,21},{6,22},{7,23},{8,24},{9,... | collective-permute-start | bytes 86024
Sparse Core Ops, SparseCore 0:
  10.3 41.7 all-gather.2
  93.9 79.7 all-gather.4
